TPU v7x, 32 devices: a whole 2x2x4 slice. The times are simulated.
32 devices in a mesh: dp: 2 (over x), expert: 16 (over z, y, core).
Axes of the slice: x: 2, y: 2, z: 4, core: 2. Of those that a mesh axis runs over, the one named last changes fastest.
Arguments:
- gradients: bfloat16 [16, 1024, 5888], P(None, ('dp', 'expert')), may hold values from -6 to 6
- momentum: bfloat16 [16, 1024, 5888], P('expert', 'dp'), may hold values from -6 to 6
- right_factor: bfloat16 [16, 5888, 256], P('expert', 'dp'), may hold values from -6 to 6
Outputs:
- new_momentum: bfloat16 [16, 1024, 5888], P('expert', 'dp')
- new_factor: bfloat16 [16, 5888, 256], P('expert', 'dp')
- update_rows: bfloat16 [16, 1024, 5888], P(None, ('dp', 'expert'))
All inputs are finite; a program needn't handle non-finite values.
Results may differ from a plain program's by a relative error of at most 0.009.
Values may be sent and summed in bfloat16 or wider, within the bound.
A program may use at most 128 MiB of HBM per device.

v0:
```python
import math
import jax
import jax.numpy as jnp
from jax import lax
from jax.sharding import PartitionSpec as P

D = 5888
FFW = 1024
RANK = 256
decay_rate = 0.95
epsilon = 1e-06


def body(gradients, momentum, right_factor):
    arrived = lax.all_to_all(gradients, "expert", split_axis=0, concat_axis=1, tiled=True)
    rank_cols = right_factor.shape[2]
    blended = (
        decay_rate * momentum[0].astype(jnp.float32) + arrived[0].astype(jnp.float32)
    ).astype(jnp.bfloat16)
    columns = blended
    left = jnp.dot(
        columns,
        lax.all_gather(right_factor[0], "dp", axis=0, tiled=True),
        preferred_element_type=jnp.float32,
    )
    gram_matrix = lax.psum(jnp.dot(left.T, left, precision=lax.Precision.HIGHEST), "dp")
    lower = jnp.linalg.cholesky(gram_matrix)
    inverse = jax.scipy.linalg.solve_triangular(
        lower, jnp.eye(rank_cols, dtype=jnp.float32), lower=True
    )
    ortho = jnp.dot(left, inverse.T, precision=lax.Precision.HIGHEST).astype(jnp.bfloat16)
    columns = blended
    right_half = lax.psum_scatter(
        lax.dot_general(
            columns, ortho, (((0,), (0,)), ((), ())), preferred_element_type=jnp.float32
        ),
        "dp",
        scatter_dimension=0,
        tiled=True,
    )
    column = lax.psum(jnp.sum(right_half * right_half, axis=0), "dp")
    own_factor = (right_half * lax.rsqrt(column / D + epsilon)).astype(jnp.bfloat16)
    right_rounded = lax.all_gather(right_half.astype(jnp.bfloat16), "dp", axis=0, tiled=True)
    full_factor = lax.all_gather(own_factor, "dp", axis=0, tiled=True)
    kept = (
        blended.astype(jnp.float32)
        - (1.0 - decay_rate)
        * lax.dot_general(
            ortho, right_rounded, (((1,), (1,)), ((), ())), preferred_element_type=jnp.float32
        )
    ).astype(jnp.bfloat16)
    update = (
        math.sqrt(FFW / RANK)
        * lax.dot_general(
            ortho, full_factor, (((1,), (1,)), ((), ())), preferred_element_type=jnp.float32
        )
    ).astype(jnp.bfloat16)
    moments = [kept]
    factors = [own_factor]
    updates = [update]
    returned = lax.all_to_all(jnp.stack(updates), "expert", split_axis=1, concat_axis=0, tiled=True)
    return (jnp.stack(moments), jnp.stack(factors), returned)


def solution(mesh):
    in_specs = (P(None, ("dp", "expert"), None), P("expert", "dp", None), P("expert", "dp", None))
    out_specs = (P("expert", "dp", None), P("expert", "dp", None), P(None, ("dp", "expert"), None))
    return jax.shard_map(body, mesh=mesh, in_specs=in_specs, out_specs=out_specs, check_vma=False)
```

profile of v0, /device:TPU:13, one launch (start us, length us, event | category | flops | bytes accessed | tf_op | source)
XLA Modules:
  0.0 616.2 jit_solution(494227464245584876)
XLA Ops:
  7.2 6.5 %all-to-all-start = ((bf16[16,32,5888]{2,1,0:T(8,128)(2,1)}), bf16[16,32,5888]{2,1,0:T(8,128)(2,1)}, u32[]{:S(2)}, u32[]{:S(2)}) async-start(bf16[16,32,5888]{2,1,0:T(8,128)(2,1)} %param.3), calls=%async_computation | async-start | bytes 12058624 | tf_op jit(solution)/shard_map/all_to_all | solution.py:15
  14.5 131.0 %all-to-all-done = bf16[16,32,5888]{2,1,0:T(8,128)(2,1)} async-done(((bf16[16,32,5888]{2,1,0:T(8,128)(2,1)}), bf16[16,32,5888]{2,1,0:T(8,128)(2,1)}, u32[]{:S(2)}, u32[]{:S(2)}) %all-to-all-start) | async-done | bytes 6029344 | tf_op jit(solution)/shard_map/all_to_all | solution.py:15
  145.5 8.9 %fusion = bf16[512,5888]{1,0:T(8,128)(2,1)} fusion(bf16[1,512,5888]{2,1,0:T(8,128)(2,1)} %param.4, bf16[16,32,5888]{2,1,0:T(8,128)(2,1)} %all-to-all-done), kind=kLoop, calls=%fused_computation.3 | loop fusion | flops 15073280 | bytes 18087936 | tf_op jit(solution)/shard_map/convert_element_type | solution.py:19
  154.3 5.3 fusion.3
  159.7 1.7 fusion.18
  161.7 22.1 %all-reduce.3.cloned.1.call-done = f32[256,256]{0,1:T(8,128)} async-done(((f32[256,256]{0,1:T(8,128)}), f32[256,256]{0,1:T(8,128)}) %all-reduce.3.cloned.1.call-update) | async-done | bytes 262160 | tf_op jit(solution)/shard_map/psum | solution.py:26
  183.8 1.1 copy.12
  184.8 1.0 fusion.8
  185.8 11.7 %cholesky.50 = f32[128,128]{1,0:T(8,128)S(1)} custom-call(f32[128,128]{1,0:T(8,128)S(1)} %cholesky.118), custom_call_target="Cholesky" | custom-call | tf_op jit(solution)/shard_map/jit(cholesky)/cholesky | solution.py:27
  197.6 9.8 %custom-call.15 = f32[1,128,128]{1,2,0:T(8,128)S(1)} custom-call(f32[1,128,128]{2,1,0:T(8,128)S(1)} %get-tuple-element.26), custom_call_target="InvertDiagBlocksLowerTriangular" | custom-call | tf_op jit(solution)/shard_map/jit(cholesky)/cholesky | solution.py:27
  207.9 11.7 %cholesky.105 = f32[128,128]{1,0:T(8,128)S(1)} custom-call(f32[128,128]{1,0:T(8,128)S(1)} %convolution_subtract_fusion.1), custom_call_target="Cholesky" | custom-call | tf_op jit(solution)/shard_map/jit(cholesky)/cholesky | solution.py:27
  219.7 0.7 compare_reduce_fusion
  221.8 4.3 while.1
  222.6 1.4 bitcast_dynamic-update-slice_fusion.2
  224.7 1.4 bitcast_dynamic-update-slice_fusion.2
  226.1 19.7 %custom-call.16 = f32[2,128,128]{1,2,0:T(8,128)S(1)} custom-call(f32[2,128,128]{2,1,0:T(8,128)S(1)} %get-tuple-element.10), custom_call_target="InvertDiagBlocksLowerTriangular" | custom-call | tf_op jit(solution)/shard_map/jit(_solve_triangular)/triangular_solve | solution.py:28
  247.3 7.1 %fusion.19 = f32[5888,256]{1,0:T(8,128)} fusion(bf16[512,5888]{1,0:T(8,128)(2,1)} %fusion, bf16[512,256]{1,0:T(8,128)(2,1)S(1)} %convolution_convert_fusion), kind=kOutput, calls=%fused_computation.47 | convolution fusion | flops 1543503872 | bytes 12320768 | tf_op jit(solution)/shard_map/dot_general | solution.py:34
  254.5 74.7 %reduce-scatter.2.cloned.1.call-done = f32[2944,256]{1,0:T(8,128)} async-done(((f32[5888,256]{1,0:T(8,128)}), f32[2944,256]{1,0:T(8,128)}) %reduce-scatter.2.cloned.1.call-update) | async-done | bytes 3014672 | tf_op jit(solution)/shard_map/reduce_scatter | solution.py:33
  329.2 2.3 multiply_reduce_fusion
  331.5 3.8 psum.15
  335.2 4.8 multiply_convert_fusion.1
  340.0 44.8 %all-gather.7.cloned.1.call-done = bf16[5888,256]{1,0:T(8,128)(2,1)} async-done(((bf16[2944,256]{1,0:T(8,128)(2,1)}), bf16[5888,256]{1,0:T(8,128)(2,1)}) %all-gather.7.cloned.1.call-update) | async-done | bytes 3014672 | tf_op jit(solution)/shard_map/all_gather | solution.py:44
  384.8 3.6 fusion.2
  388.4 10.8 %copy.17 = bf16[1,512,5888]{2,0,1:T(2,128)(2,1)} copy(bf16[1,512,5888]{2,1,0:T(8,128)(2,1)S(1)} %fusion.2) | data formatting | bytes 12058624 | tf_op jit(solution)/shard_map/stack | solution.py:61
  399.8 38.3 %reduce.12 = bf16[512,5888]{1,0:T(8,128)(2,1)} reduce(bf16[512,1,5888]{2,1,0:T(2,128)(2,1)} %bitcast.60, bf16[]{:T(256)} %broadcast.118), dimensions={1}, to_apply=%bitcast.52.reduce_sub_computation | reduce | bytes 12058626
  438.1 11.3 %reshape.59 = bf16[16,2,94208]{2,1,0:T(2,128)(2,1)} reshape(bf16[512,5888]{1,0:T(8,128)(2,1)} %reduce.12) | data formatting | bytes 12058624
  449.5 6.5 %all-to-all-start.1 = ((bf16[16,2,94208]{2,1,0:T(2,128)(2,1)}), bf16[16,2,94208]{2,1,0:T(2,128)(2,1)}, u32[]{:S(2)}, u32[]{:S(2)}) async-start(bf16[16,2,94208]{2,1,0:T(2,128)(2,1)} %reshape.59), calls=%async_computation.2 | async-start | bytes 12058624 | tf_op jit(solution)/shard_map/all_to_all | solution.py:61
  456.6 44.4 %all-gather.5.cloned.1.call-done = bf16[5888,256]{1,0:T(8,128)(2,1)} async-done(((bf16[2944,256]{1,0:T(8,128)(2,1)}), bf16[5888,256]{1,0:T(8,128)(2,1)}) %all-gather.5.cloned.1.call-update) | async-done | bytes 3014672 | tf_op jit(solution)/shard_map/all_gather | solution.py:43
  501.0 8.0 %fusion.1 = bf16[1,512,5888]{2,1,0:T(8,128)(2,1)} fusion(bf16[512,256]{1,0:T(8,128)(2,1)S(1)} %convolution_convert_fusion, bf16[5888,256]{1,0:T(8,128)(2,1)} %all-gather.5.cloned.1.call-done, bf16[512,5888]{1,0:T(8,128)(2,1)} %fusion), kind=kOutput, calls=%fused_computation.6 | convolution fusion | flops 1555562496 | bytes 15335424 | tf_op jit(solution)/shard_map/dot_general | solution.py:48
  509.0 78.8 %all-to-all-done.1 = bf16[16,2,94208]{2,1,0:T(2,128)(2,1)} async-done(((bf16[16,2,94208]{2,1,0:T(2,128)(2,1)}), bf16[16,2,94208]{2,1,0:T(2,128)(2,1)}, u32[]{:S(2)}, u32[]{:S(2)}) %all-to-all-start.1) | async-done | bytes 6029344 | tf_op jit(solution)/shard_map/all_to_all | solution.py:61
  587.8 14.0 %reshape.60 = bf16[512,1,5888]{2,1,0:T(2,128)(2,1)} reshape(bf16[16,2,94208]{2,1,0:T(2,128)(2,1)} %all-to-all-done.1) | data formatting | bytes 12058624
  601.8 7.9 %copy.15 = bf16[1,512,5888]{2,1,0:T(8,128)(2,1)} copy(bf16[1,512,5888]{2,0,1:T(2,128)(2,1)} %bitcast.59) | data formatting | bytes 12058624
  (32 shorter events, 5.6 us)
Async XLA Ops:
  7.2 138.3 %all-to-all-start = ((bf16[16,32,5888]{2,1,0:T(8,128)(2,1)}), bf16[16,32,5888]{2,1,0:T(8,128)(2,1)}, u32[]{:S(2)}, u32[]{:S(2)}) async-start(bf16[16,32,5888]{2,1,0:T(8,128)(2,1)} %param.3), calls=%async_computation | async-start | bytes 12058624 | tf_op jit(solution)/shard_map/all_to_all | solution.py:15
  13.7 140.6 %all-gather.9.cloned.1.call-start = ((), (), s32[]{:S(2)}) async-start(), calls=%async_computation.7 | async-start | bytes 4521984 | tf_op jit(solution)/shard_map/all_gather | solution.py:23
  14.4 169.3 %all-reduce.3.cloned.1.call-start = ((), (), s32[]{:S(2)}) async-start(), calls=%async_computation.3 | async-start | bytes 524288 | tf_op jit(solution)/shard_map/psum | solution.py:26
  161.4 167.8 %reduce-scatter.2.cloned.1.call-start = ((), (), s32[]{:S(2)}) async-start(), calls=%async_computation.4 | async-start | bytes 9043968 | tf_op jit(solution)/shard_map/reduce_scatter | solution.py:33
  254.4 130.4 %all-gather.7.cloned.1.call-start = ((), (), s32[]{:S(2)}) async-start(), calls=%async_computation.6 | async-start | bytes 4521984 | tf_op jit(solution)/shard_map/all_gather | solution.py:44
  449.5 138.3 %all-to-all-start.1 = ((bf16[16,2,94208]{2,1,0:T(2,128)(2,1)}), bf16[16,2,94208]{2,1,0:T(2,128)(2,1)}, u32[]{:S(2)}, u32[]{:S(2)}) async-start(bf16[16,2,94208]{2,1,0:T(2,128)(2,1)} %reshape.59), calls=%async_computation.2 | async-start | bytes 12058624 | tf_op jit(solution)/shard_map/all_to_all | solution.py:61
  456.0 45.0 %all-gather.5.cloned.1.call-start = ((), (), s32[]{:S(2)}) async-start(), calls=%async_computation.5 | async-start | bytes 4521984 | tf_op jit(solution)/shard_map/all_gather | solution.py:43
Sparse Core Ops, SparseCore 0:
  16.0 43.8 all-gather.8
  161.5 22.1 all-reduce.2
  254.5 74.6 reduce-scatter.1
  340.2 44.5 all-gather.6
  458.0 42.9 all-gather.4
where the time goes:
time: 617 us; the launch traced here: 616 us
  waiting for transfers between devices  397 us (64%)
  other arithmetic  109 us (18%)
  local copies, waits for them, and re-layouts  49.9 us (8%)
  matrix products  27.7 us (4%)
  between operations  15.3 us (2%)
  starting transfers between devices  13.7 us (2%)
    all_to_all x1, waiting for transfers between devices, body(): lax.all_to_all(gradients, 'expert', split_axis=0, concat_axis=1, tiled=True)  131 us
    all_to_all x1, waiting for transfers between devices, body(): lax.all_to_all(jnp.stack(updates), 'expert', split_axis=1, concat_axis=0,...  78.8 us
    reduce_scatter x1, waiting for transfers between devices, body(): lax.psum_scatter(lax.dot_general(columns, ortho, (((0,), (0,)), ((), ()))...  74.7 us
    all_gather x1, waiting for transfers between devices, body(): full_factor = lax.all_gather(own_factor, 'dp', axis=0, tiled=True)  44.8 us
    all_gather x1, waiting for transfers between devices, body(): lax.all_gather(right_half.astype(jnp.bfloat16), 'dp', axis=0, tiled=True)  44.4 us
    unnamed x2, other arithmetic  38.3 us
    another operation x6, other arithmetic, body(): lower = jnp.linalg.cholesky(gram_matrix)  34 us
    unnamed x4, local copies, waits for them, and re-layouts  33.8 us
  transfers between devices with their start and end apart: 7, of which 6 were waited for; matrix products, arithmetic and copies ran while one was open for 3% of the time, Pallas kernels for 0%

commit v1 on v0

--- a/solution.py
+++ b/solution.py
@@ -41,7 +41,12 @@
     column = lax.psum(jnp.sum(right_half * right_half, axis=0), "dp")
     own_factor = (right_half * lax.rsqrt(column / D + epsilon)).astype(jnp.bfloat16)
     right_rounded = lax.all_gather(right_half.astype(jnp.bfloat16), "dp", axis=0, tiled=True)
-    full_factor = lax.all_gather(own_factor, "dp", axis=0, tiled=True)
+    full_factor = jnp.concatenate(
+        jax.lax.all_to_all(
+            jnp.stack([own_factor for _ in range(jax.lax.axis_size("dp"))], 0), "dp", 0, 0
+        ),
+        0,
+    )
     kept = (
         blended.astype(jnp.float32)
         - (1.0 - decay_rate)

time: 617 us -> 608 us (0.985)
  waiting for transfers between devices: 397 us -> 352 us
  blocking collectives: 3.77 us -> 39.2 us
    all_gather x1 -> x0, waiting for transfers between devices: 44.8 us -> none  [body(): full_factor = lax.all_gather(own_factor, 'dp', axis=0, tiled=True)]
    all_to_all x0 -> x1, blocking collectives: none -> 35.4 us  [body(): jax.lax.all_to_all(jnp.stack([own_factor for _ in range(jax.lax.axis_size...]
    unnamed x4 -> x6, local copies, waits for them, and re-layouts: 33.8 us -> 33.8 us
  transfers between devices with their start and end apart: 7 -> 6, of which waited for: 6 -> 5; matrix products, arithmetic and copies ran while one was open for 3% -> 3% of each run, Pallas kernels for 0% -> 0%
where the time goes in v1:
time: 608 us; the launch traced here: 607 us
  waiting for transfers between devices  352 us (58%)
  other arithmetic  109 us (18%)
  local copies, waits for them, and re-layouts  49.9 us (8%)
  blocking collectives  39.2 us (6%)
  matrix products  25.8 us (4%)
  starting transfers between devices  15.4 us (3%)
  between operations  15.3 us (3%)
    all_to_all x1, waiting for transfers between devices, body(): lax.all_to_all(gradients, 'expert', split_axis=0, concat_axis=1, tiled=True)  131 us
    all_to_all x1, waiting for transfers between devices, body(): lax.all_to_all(jnp.stack(updates), 'expert', split_axis=1, concat_axis=0,...  78.8 us
    reduce_scatter x1, waiting for transfers between devices, body(): lax.psum_scatter(lax.dot_general(columns, ortho, (((0,), (0,)), ((), ()))...  74.8 us
    all_gather x1, waiting for transfers between devices, body(): lax.all_gather(right_half.astype(jnp.bfloat16), 'dp', axis=0, tiled=True)  44.4 us
    unnamed x2, other arithmetic  38.3 us
    all_to_all x1, blocking collectives, body(): jax.lax.all_to_all(jnp.stack([own_factor for _ in range(jax.lax.axis_size...  35.4 us
    another operation x6, other arithmetic, body(): lower = jnp.linalg.cholesky(gram_matrix)  34 us
    unnamed x6, local copies, waits for them, and re-layouts  33.8 us
  transfers between devices with their start and end apart: 6, of which 5 were waited for; matrix products, arithmetic and copies ran while one was open for 3% of the time, Pallas kernels for 0%

profile of v1, /device:TPU:13, one launch (start us, length us, event | category | flops | bytes accessed | tf_op | source)
XLA Modules:
  0.0 606.8 jit_solution(17346674337146529898)
XLA Ops:
  7.2 6.5 %all-to-all-start = ((bf16[16,32,5888]{2,1,0:T(8,128)(2,1)}), bf16[16,32,5888]{2,1,0:T(8,128)(2,1)}, u32[]{:S(2)}, u32[]{:S(2)}) async-start(bf16[16,32,5888]{2,1,0:T(8,128)(2,1)} %param.3), calls=%async_computation | async-start | bytes 12058624 | tf_op jit(solution)/shard_map/all_to_all | solution.py:15
  14.5 131.0 %all-to-all-done = bf16[16,32,5888]{2,1,0:T(8,128)(2,1)} async-done(((bf16[16,32,5888]{2,1,0:T(8,128)(2,1)}), bf16[16,32,5888]{2,1,0:T(8,128)(2,1)}, u32[]{:S(2)}, u32[]{:S(2)}) %all-to-all-start) | async-done | bytes 6029344 | tf_op jit(solution)/shard_map/all_to_all | solution.py:15
  145.5 8.9 %fusion = bf16[512,5888]{1,0:T(8,128)(2,1)} fusion(bf16[1,512,5888]{2,1,0:T(8,128)(2,1)} %param.4, bf16[16,32,5888]{2,1,0:T(8,128)(2,1)} %all-to-all-done), kind=kLoop, calls=%fused_computation.3 | loop fusion | flops 15073280 | bytes 18087936 | tf_op jit(solution)/shard_map/convert_element_type | solution.py:19
  154.3 5.3 fusion.3
  159.7 1.7 fusion.19
  161.7 22.1 %all-reduce.3.cloned.1.call-done = f32[256,256]{0,1:T(8,128)} async-done(((f32[256,256]{0,1:T(8,128)}), f32[256,256]{0,1:T(8,128)}) %all-reduce.3.cloned.1.call-update) | async-done | bytes 262160 | tf_op jit(solution)/shard_map/psum | solution.py:26
  183.8 1.1 copy.12
  184.8 1.0 fusion.9
  185.8 11.7 %cholesky.50 = f32[128,128]{1,0:T(8,128)S(1)} custom-call(f32[128,128]{1,0:T(8,128)S(1)} %cholesky.118), custom_call_target="Cholesky" | custom-call | tf_op jit(solution)/shard_map/jit(cholesky)/cholesky | solution.py:27
  197.6 9.8 %custom-call.15 = f32[1,128,128]{1,2,0:T(8,128)S(1)} custom-call(f32[1,128,128]{2,1,0:T(8,128)S(1)} %get-tuple-element.26), custom_call_target="InvertDiagBlocksLowerTriangular" | custom-call | tf_op jit(solution)/shard_map/jit(cholesky)/cholesky | solution.py:27
  207.9 11.7 %cholesky.105 = f32[128,128]{1,0:T(8,128)S(1)} custom-call(f32[128,128]{1,0:T(8,128)S(1)} %convolution_subtract_fusion.1), custom_call_target="Cholesky" | custom-call | tf_op jit(solution)/shard_map/jit(cholesky)/cholesky | solution.py:27
  219.7 0.7 compare_reduce_fusion
  221.8 4.3 while.1
  222.6 1.4 bitcast_dynamic-update-slice_fusion.2
  224.7 1.4 bitcast_dynamic-update-slice_fusion.2
  226.1 19.7 %custom-call.16 = f32[2,128,128]{1,2,0:T(8,128)S(1)} custom-call(f32[2,128,128]{2,1,0:T(8,128)S(1)} %get-tuple-element.10), custom_call_target="InvertDiagBlocksLowerTriangular" | custom-call | tf_op jit(solution)/shard_map/jit(_solve_triangular)/triangular_solve | solution.py:28
  247.3 7.1 %fusion.20 = f32[5888,256]{1,0:T(8,128)} fusion(bf16[512,5888]{1,0:T(8,128)(2,1)} %fusion, bf16[512,256]{1,0:T(8,128)(2,1)S(1)} %convolution_convert_fusion), kind=kOutput, calls=%fused_computation.49 | convolution fusion | flops 1543503872 | bytes 12320768 | tf_op jit(solution)/shard_map/dot_general | solution.py:34
  254.4 74.8 %reduce-scatter.2.cloned.1.call-done = f32[2944,256]{1,0:T(8,128)} async-done(((f32[5888,256]{1,0:T(8,128)}), f32[2944,256]{1,0:T(8,128)}) %reduce-scatter.2.cloned.1.call-update) | async-done | bytes 3014672 | tf_op jit(solution)/shard_map/reduce_scatter | solution.py:33
  329.2 2.3 multiply_reduce_fusion
  331.5 3.8 psum.15
  335.2 4.3 fusion.5
  339.8 35.4 %all_to_all.26 = bf16[2,2944,256]{2,1,0:T(8,128)(2,1)S(1)} all-to-all(bf16[2,2944,256]{2,1,0:T(8,128)(2,1)S(1)} %pad_maximum_fusion), channel_id=1, replica_groups=mesh['dp'=2,'expert'=16] {'dp'}, dimensions={0} | all-to-all | bytes 6029312 | tf_op jit(solution)/shard_map/all_to_all | solution.py:45
  375.2 1.8 fusion.2
  377.0 10.8 %copy.17 = bf16[1,512,5888]{2,0,1:T(2,128)(2,1)} copy(bf16[1,512,5888]{2,1,0:T(8,128)(2,1)S(1)} %fusion.2) | data formatting | bytes 12058624 | tf_op jit(solution)/shard_map/stack | solution.py:66
  388.4 38.3 %reduce.12 = bf16[512,5888]{1,0:T(8,128)(2,1)} reduce(bf16[512,1,5888]{2,1,0:T(2,128)(2,1)} %bitcast.62, bf16[]{:T(256)} %broadcast.118), dimensions={1}, to_apply=%bitcast.54.reduce_sub_computation | reduce | bytes 12058626
  426.7 11.3 %reshape.63 = bf16[16,2,94208]{2,1,0:T(2,128)(2,1)} reshape(bf16[512,5888]{1,0:T(8,128)(2,1)} %reduce.12) | data formatting | bytes 12058624
  438.1 8.5 %all-to-all-start.2 = ((bf16[16,2,94208]{2,1,0:T(2,128)(2,1)}), bf16[16,2,94208]{2,1,0:T(2,128)(2,1)}, u32[]{:S(2)}, u32[]{:S(2)}) async-start(bf16[16,2,94208]{2,1,0:T(2,128)(2,1)} %reshape.63), calls=%async_computation.3 | async-start | bytes 12058624 | tf_op jit(solution)/shard_map/all_to_all | solution.py:66
  447.2 44.4 %all-gather.4.cloned.1.call-done = bf16[5888,256]{1,0:T(8,128)(2,1)} async-done(((bf16[2944,256]{1,0:T(8,128)(2,1)}), bf16[5888,256]{1,0:T(8,128)(2,1)}) %all-gather.4.cloned.1.call-update) | async-done | bytes 3014672 | tf_op jit(solution)/shard_map/all_gather | solution.py:43
  491.6 8.0 %fusion.1 = bf16[1,512,5888]{2,1,0:T(8,128)(2,1)} fusion(bf16[512,256]{1,0:T(8,128)(2,1)S(1)} %convolution_convert_fusion, bf16[5888,256]{1,0:T(8,128)(2,1)} %all-gather.4.cloned.1.call-done, bf16[512,5888]{1,0:T(8,128)(2,1)} %fusion), kind=kOutput, calls=%fused_computation.6 | convolution fusion | flops 1555562496 | bytes 15335424 | tf_op jit(solution)/shard_map/dot_general | solution.py:53
  499.6 78.8 %all-to-all-done.2 = bf16[16,2,94208]{2,1,0:T(2,128)(2,1)} async-done(((bf16[16,2,94208]{2,1,0:T(2,128)(2,1)}), bf16[16,2,94208]{2,1,0:T(2,128)(2,1)}, u32[]{:S(2)}, u32[]{:S(2)}) %all-to-all-start.2) | async-done | bytes 6029344 | tf_op jit(solution)/shard_map/all_to_all | solution.py:66
  578.4 14.0 %reshape.64 = bf16[512,1,5888]{2,1,0:T(2,128)(2,1)} reshape(bf16[16,2,94208]{2,1,0:T(2,128)(2,1)} %all-to-all-done.2) | data formatting | bytes 12058624
  592.4 7.9 %copy.15 = bf16[1,512,5888]{2,1,0:T(8,128)(2,1)} copy(bf16[1,512,5888]{2,0,1:T(2,128)(2,1)} %bitcast.61) | data formatting | bytes 12058624
  (33 shorter events, 5.8 us)
Async XLA Ops:
  7.2 138.3 %all-to-all-start = ((bf16[16,32,5888]{2,1,0:T(8,128)(2,1)}), bf16[16,32,5888]{2,1,0:T(8,128)(2,1)}, u32[]{:S(2)}, u32[]{:S(2)}) async-start(bf16[16,32,5888]{2,1,0:T(8,128)(2,1)} %param.3), calls=%async_computation | async-start | bytes 12058624 | tf_op jit(solution)/shard_map/all_to_all | solution.py:15
  13.7 140.6 %all-gather.6.cloned.1.call-start = ((), (), s32[]{:S(2)}) async-start(), calls=%async_computation.7 | async-start | bytes 4521984 | tf_op jit(solution)/shard_map/all_gather | solution.py:23
  14.4 169.3 %all-reduce.3.cloned.1.call-start = ((), (), s32[]{:S(2)}) async-start(), calls=%async_computation.4 | async-start | bytes 524288 | tf_op jit(solution)/shard_map/psum | solution.py:26
  161.4 167.8 %reduce-scatter.2.cloned.1.call-start = ((), (), s32[]{:S(2)}) async-start(), calls=%async_computation.5 | async-start | bytes 9043968 | tf_op jit(solution)/shard_map/reduce_scatter | solution.py:33
  339.6 37.4 %copy-start = (bf16[1,2944,256]{2,1,0:T(8,128)(2,1)}, bf16[1,2944,256]{2,1,0:T(8,128)(2,1)S(1)}, u32[]{:S(2)}) copy-start(bf16[1,2944,256]{2,1,0:T(8,128)(2,1)S(1)} %get-tuple-element.21) | copy-start | bytes 4521988
  438.1 140.3 %all-to-all-start.2 = ((bf16[16,2,94208]{2,1,0:T(2,128)(2,1)}), bf16[16,2,94208]{2,1,0:T(2,128)(2,1)}, u32[]{:S(2)}, u32[]{:S(2)}) async-start(bf16[16,2,94208]{2,1,0:T(2,128)(2,1)} %reshape.63), calls=%async_computation.3 | async-start | bytes 12058624 | tf_op jit(solution)/shard_map/all_to_all | solution.py:66
  446.6 45.0 %all-gather.4.cloned.1.call-start = ((), (), s32[]{:S(2)}) async-start(), calls=%async_computation.6 | async-start | bytes 4521984 | tf_op jit(solution)/shard_map/all_gather | solution.py:43
Sparse Core Ops, SparseCore 0:
  16.0 43.8 all-gather.5
  161.5 22.1 all-reduce.2
  254.5 74.6 reduce-scatter.1
  448.6 42.9 all-gather.3
